TPU v7x, 32 devices: a whole 2x2x4 slice. The times are simulated.
32 devices in a mesh: dp: 4 (over x, core), fsdp: 4 (over z), tp: 2 (over y).
Axes of the slice: x: 2, y: 2, z: 4, core: 2. Of those that a mesh axis runs over, the one named last changes fastest.
Arguments:
- hidden: bfloat16 [8192, 7168], P(('dp', 'fsdp')), may hold values from -6 to 6
- cotangent: bfloat16 [8192, 576], P(('dp', 'fsdp'), 'tp'), may hold values from -6 to 6
- rewards: int32 [64], P(('dp', 'fsdp')), may hold values from 0 to 8
- groups: int32 [64], P(('dp', 'fsdp')), may hold values from 0 to 3, as said below
- lengths: int32 [64], P(('dp', 'fsdp')), may hold values from 1 to 128
- master: float32 [4, 1792, 576], P('fsdp', 'dp', 'tp'), may hold values from -6 to 6
Outputs:
- grad_owned: float32 [4, 1792, 576], P('fsdp', 'dp', 'tp')
- rollout: bfloat16 [4, 1792, 576], P('fsdp')
Inputs may be any that keep to these rules, and one draw needn't show every extreme that they name: `groups`: each prompt number names exactly 16 samples.
All inputs are finite; a program needn't handle non-finite values.
Results may differ from a plain program's by a relative error of at most 0.0033.
Values may be sent and summed in bfloat16 or wider, within the bound.
A program may use at most 64 MiB of HBM per device.

v0:
```python
import jax
import jax.numpy as jnp
from jax import lax
from jax.sharding import PartitionSpec as P

D = 7168
GROUP = 16


def exact_dot(left, right):
    return jnp.dot(left, right, precision=lax.Precision.HIGHEST)


def shards(hidden, cotangent, rewards, groups, lengths, master):
    fsdp_size = lax.axis_size("fsdp")
    dp_size = lax.axis_size("dp")
    samp_local = rewards.shape[0]
    group_count = samp_local * dp_size * fsdp_size // GROUP
    labels = jnp.arange(group_count, dtype=jnp.int32)
    reward_f = rewards.astype(jnp.float32)
    local_onehot = (groups[:, None] == labels[None, :]).astype(jnp.float32)
    totals, squares = lax.psum(
        (exact_dot(reward_f, local_onehot), exact_dot(reward_f * reward_f, local_onehot)),
        ("dp", "fsdp"),
    )
    group_mean = totals / GROUP
    group_square = squares / GROUP
    sample_mean = exact_dot(local_onehot, group_mean)
    sample_square = exact_dot(local_onehot, group_square)
    advantage = (reward_f - sample_mean) / jnp.sqrt(sample_square - sample_mean * sample_mean + 1.0)
    seq_len = hidden.shape[0] // samp_local
    positions = jnp.arange(seq_len, dtype=jnp.int32)
    live = (positions[None, :] < lengths[:, None]).astype(jnp.float32)
    scale = (advantage[:, None] * live / lengths[:, None].astype(jnp.float32)).reshape(
        hidden.shape[0]
    )
    weighted = (cotangent.astype(jnp.float32) * scale[:, None]).astype(jnp.bfloat16)
    cols_local = cotangent.shape[1]
    block_rows = D // fsdp_size
    product = jnp.einsum("td,tc->dc", hidden, weighted, preferred_element_type=jnp.float32)
    reduced = lax.psum_scatter(
        product.reshape(1 * lax.axis_size("fsdp"), block_rows, cols_local),
        "fsdp",
        scatter_dimension=0,
        tiled=True,
    )
    owned = lax.psum_scatter(reduced, "dp", scatter_dimension=1, tiled=True)
    updated = (master - 0.1 * owned).astype(jnp.bfloat16)
    full_rows = lax.all_gather(updated, "tp", axis=2, tiled=True)
    rollout = lax.all_gather(full_rows, "dp", axis=1, tiled=True)
    return (owned, rollout)


def solution(mesh):
    placed = (
        P(("dp", "fsdp"), None),
        P(("dp", "fsdp"), "tp"),
        P(("dp", "fsdp")),
        P(("dp", "fsdp")),
        P(("dp", "fsdp")),
        P("fsdp", "dp", "tp"),
    )
    return jax.shard_map(
        shards,
        mesh=mesh,
        in_specs=placed,
        out_specs=(P("fsdp", "dp", "tp"), P("fsdp", None, None)),
        check_vma=False,
    )
```

profile of v0, /device:TPU:0, one launch (start us, length us, event | category | flops | bytes accessed | tf_op | source)
XLA Modules:
  0.0 288.7 jit_solution(1073819493120630368)
XLA Ops:
  7.2 0.0 reduce-scatter.5.cloned.1.call-start
  7.2 0.9 convolution_bitcast_fusion.1
  8.1 0.9 convolution_bitcast_fusion.3
  8.9 0.7 convert_element_type.20
  9.6 35.1 %all-reduce = (f32[4]{0:T(128)S(1)}, f32[4]{0:T(128)S(1)}) all-reduce(f32[4]{0:T(128)S(1)} %convolution_bitcast_fusion.3, f32[4]{0:T(128)S(1)} %convolution_bitcast_fusion.1), channel_id=1, replica_groups=mesh['dp'=4,'fsdp'=4,'tp'=2] {'dp','fsdp'}, use_global_device_ids=true, to_apply=%region_0.0 | all-reduce | flops 8 | bytes 64 | tf_op jit(solution)/shard_map/psum | solution.py:22
  44.7 0.8 convolution_bitcast_fusion.2
  45.6 0.9 fusion.3
  46.4 0.7 divide_bitcast_fusion
  47.2 5.5 %fusion.4 = f32[288,7168]{1,0:T(8,128)S(1)} fusion(bf16[512,7168]{1,0:T(8,128)(2,1)} %param.6, bf16[512,288]{0,1:T(8,128)(2,1)} %param.7, f32[512]{0:T(512)S(1)} %divide_bitcast_fusion), kind=kOutput, calls=%fused_computation.13 | convolution fusion | flops 2114371584 | bytes 15894528 | tf_op jit(solution)/shard_map/td,tc->dc/dot_general | solution.py:40
  52.7 3.8 %copy.18 = f32[36,4,8,1792]{3,2,0,1:T(8,128)} copy(f32[36,4,8,1792]{3,2,1,0:T(8,128)S(1)} %bitcast.43) | data formatting | bytes 16515072 | tf_op jit(solution)/shard_map/reshape | solution.py:42
  56.5 0.0 reduce-scatter.5.cloned.1.call-update
  56.5 0.0 copy-start.1
  56.6 0.0 reduce-scatter.7.cloned.1.call-start
  56.6 139.9 %reduce-scatter.5.cloned.1.call-done = f32[1,1792,288]{1,2,0:T(8,128)} async-done(((f32[4,1792,288]{1,2,0:T(8,128)}), f32[1,1792,288]{1,2,0:T(8,128)}) %reduce-scatter.5.cloned.1.call-update) | async-done | bytes 2064400 | tf_op jit(solution)/shard_map/reduce_scatter | solution.py:41
  196.5 6.9 %copy.12 = f32[1,1792,288]{2,0,1:T(1,128)S(1)} copy(f32[1,1792,288]{1,2,0:T(8,128)} %reduce-scatter.5.cloned.1.call-done) | data formatting | bytes 4128768
  203.4 1.7 copy.19
  205.1 0.0 reduce-scatter.7.cloned.1.call-update
  205.1 0.0 all-gather.2.cloned.1.call-start
  205.2 36.0 %reduce-scatter.7.cloned.1.call-done = f32[448,288]{1,0:T(8,128)} async-done(((f32[1792,288]{1,0:T(8,128)}), f32[448,288]{1,0:T(8,128)}) %reduce-scatter.7.cloned.1.call-update) | async-done | bytes 516112
  241.2 1.6 reshape_bitcast_fusion
  242.8 1.0 copy.13
  243.8 0.0 copy-done.1
  243.8 0.0 copy-start
  243.8 0.1 subtract_convert_fusion
  243.9 9.2 %all_gather.6 = bf16[1,448,576]{1,2,0:T(8,128)(2,1)S(1)} all-gather(bf16[1,448,288]{1,2,0:T(8,128)(2,1)S(1)} %subtract_convert_fusion), channel_id=1, replica_groups=mesh['dp'=4,'fsdp'=4,'tp'=2] {'tp'}, dimensions={2}, use_global_device_ids=true | all-gather | bytes 774144 | tf_op jit(solution)/shard_map/all_gather | solution.py:49
  253.2 1.1 copy.10
  254.2 0.0 all-gather.2.cloned.1.call-update
  254.3 23.8 %all-gather.2.cloned.1.call-done = bf16[1,1792,576]{2,1,0:T(8,128)(2,1)} async-done(((bf16[1,448,576]{2,1,0:T(8,128)(2,1)}), bf16[1,1792,576]{2,1,0:T(8,128)(2,1)}) %all-gather.2.cloned.1.call-update) | async-done | bytes 2064400 | tf_op jit(solution)/shard_map/all_gather | solution.py:50
  278.1 4.1 %copy.11 = bf16[1,1792,576]{1,2,0:T(8,128)(2,1)} copy(bf16[1,1792,576]{2,1,0:T(8,128)(2,1)} %all-gather.2.cloned.1.call-done) | data formatting | bytes 4128768
  282.2 0.0 copy-done
Async XLA Ops:
  7.2 189.3 %reduce-scatter.5.cloned.1.call-start = ((), (), s32[]{:S(2)}) async-start(), calls=%async_computation.2 | async-start | bytes 10321920 | tf_op jit(solution)/shard_map/reduce_scatter | solution.py:41
  56.5 187.2 %copy-start.1 = (f32[1,448,288]{1,2,0:T(8,128)S(1)}, f32[1,448,288]{1,2,0:T(8,128)}, u32[]{:S(2)}) copy-start(f32[1,448,288]{1,2,0:T(8,128)} %param.11) | copy-start | bytes 1548292
  56.6 184.6 %reduce-scatter.7.cloned.1.call-start = ((), (), s32[]{:S(2)}) async-start(), calls=%async_computation.4 | async-start | bytes 3440640
  205.1 73.0 %all-gather.2.cloned.1.call-start = ((), (), s32[]{:S(2)}) async-start(), calls=%async_computation.3 | async-start | bytes 2867200 | tf_op jit(solution)/shard_map/all_gather | solution.py:50
  243.8 38.4 %copy-start = (f32[1,448,288]{1,2,0:T(8,128)}, f32[1,448,288]{1,2,0:T(8,128)S(1)}, u32[]{:S(2)}) copy-start(f32[1,448,288]{1,2,0:T(8,128)S(1)} %copy.13) | copy-start | bytes 1548292
Sparse Core Ops, SparseCore 0:
  56.7 139.7 reduce-scatter.4
  205.2 35.8 reduce-scatter.6
  254.4 23.6 all-gather.1
where the time goes:
time: 289 us
  waiting for transfers between devices  200 us (69%)
  blocking collectives  44.4 us (15%)
  local copies, waits for them, and re-layouts  20.2 us (7%)
  between operations  13.8 us (5%)
  matrix products  8.94 us (3%)
    reduce_scatter x1, waiting for transfers between devices, shards(): lax.psum_scatter(product.reshape(1 * lax.axis_size('fsdp'), block_rows, c...  140 us
    unnamed x4, waiting for transfers between devices  36.1 us
    psum x1, blocking collectives, shards(): lax.psum((exact_dot(reward_f, local_onehot), exact_dot(reward_f * reward_...  35.1 us
    all_gather x1, waiting for transfers between devices, shards(): rollout = lax.all_gather(full_rows, 'dp', axis=1, tiled=True)  23.8 us
    unnamed x9, local copies, waits for them, and re-layouts  15.3 us
    all_gather x1, blocking collectives, shards(): full_rows = lax.all_gather(updated, 'tp', axis=2, tiled=True)  9.24 us
  transfers between devices with their start and end apart: 3, of which 3 were waited for; matrix products, arithmetic and copies ran while one was open for 0% of the time, Pallas kernels for 0%

commit v1 on v0

--- a/solution.py
+++ b/solution.py
@@ -1,6 +1,10 @@
+import functools
+
 import jax
 import jax.numpy as jnp
 from jax import lax
+from jax.experimental import pallas as pl
+from jax.experimental.pallas import tpu as pltpu
 from jax.sharding import PartitionSpec as P
 
 D = 7168
@@ -51,6 +55,279 @@
     return (owned, rollout)
 
 
+OFFSETS = (2, 3, 1, 0)
+LANES = 128
+MESH = pl.DeviceIdType.MESH
+
+
+def fused_kernel(
+    n_dp, n_fsdp, n_tp,
+    rewards_ref, groups_ref, lengths_ref, hidden_ref, cot_ref, master_ref,
+    grad_ref, roll_ref,
+    hid, cot, mast, cot_t, scaled, stats, mine, pair_out, pair_in, x_mine, x_out, x_in,
+    z_out, z_in, mast_t, full, full_t, gathered,
+    hid_sem, cot_sem, mast_sem, st_send, st_recv, m_send, m_recv, p_send, p_recv,
+    x_send, x_recv, z_send, z_recv, f_send, f_recv, g_send, g_recv,
+):
+    dp, z, y = lax.axis_index("dp"), lax.axis_index("fsdp"), lax.axis_index("tp")
+    x, c = dp // 2, dp % 2
+    sibling = {"dp": x * 2 + (1 - c), "fsdp": z, "tp": y}
+    x_next = {"dp": (1 - x) * 2 + c, "fsdp": z, "tp": y}
+    y_next = {"dp": dp, "fsdp": z, "tp": 1 - y}
+    samples = rewards_ref.shape[0]
+    tokens, cols = cot.shape
+    half = cols // 2
+    seq = tokens // samples
+    chunk = hid.shape[2]
+    pair = chunk // 2
+    own_rows = pair // 2
+
+    def remote(src, dst, send, recv, where):
+        return pltpu.make_async_remote_copy(
+            src_ref=src, dst_ref=dst, send_sem=send, recv_sem=recv,
+            device_id=where, device_id_type=MESH,
+        )
+
+    peers = [
+        (i * n_fsdp + j, {"dp": (dp + i) % n_dp, "fsdp": (z + j) % n_fsdp, "tp": y})
+        for i in range(n_dp) for j in range(n_fsdp) if i or j
+    ]
+    barrier = pltpu.get_barrier_semaphore()
+    for _, where in peers:
+        pl.semaphore_signal(barrier, inc=1, device_id=where, device_id_type=MESH)
+    pl.semaphore_signal(barrier, inc=1, device_id=y_next, device_id_type=MESH)
+
+    cot_copy = pltpu.make_async_copy(cot_ref, cot, cot_sem)
+    cot_copy.start()
+    hid_copies = []
+    for k, off in enumerate(OFFSETS):
+        start = pl.multiple_of(((z + off) % n_fsdp) * chunk, LANES)
+        hid_copies.append(
+            pltpu.make_async_copy(hidden_ref.at[:, pl.ds(start, chunk)], hid.at[k], hid_sem.at[k])
+        )
+        hid_copies[-1].start()
+    mast_copy = pltpu.make_async_copy(master_ref.at[0], mast.at[c], mast_sem)
+    mast_copy.start()
+
+    lane = lax.broadcasted_iota(jnp.int32, (1, LANES), 1)
+    total_row = jnp.zeros((1, LANES), jnp.float32)
+    square_row = jnp.zeros((1, LANES), jnp.float32)
+    for s in range(samples):
+        reward = rewards_ref[s].astype(jnp.float32)
+        hit = lane == groups_ref[s]
+        total_row += jnp.where(hit, reward, 0.0)
+        square_row += jnp.where(hit, reward * reward, 0.0)
+    row = lax.broadcasted_iota(jnp.int32, (8, LANES), 0)
+    stats[0] = jnp.where(row == 0, total_row, jnp.where(row == 1, square_row, 0.0))
+
+    pl.semaphore_wait(barrier, len(peers) + 1)
+    stat_copies = []
+    for slot, where in peers:
+        stat_copies.append(remote(stats.at[0], stats.at[slot], st_send.at[slot], st_recv.at[slot], where))
+        stat_copies[-1].start()
+
+    cot_copy.wait()
+    cot_t[...] = cot[...].astype(jnp.float32).T
+    for copy in stat_copies:
+        copy.wait_recv()
+    summed = stats[0]
+    for slot, _ in peers:
+        summed += stats[slot]
+    totals, squares = summed[0:1], summed[1:2]
+    for s in range(samples):
+        reward = rewards_ref[s].astype(jnp.float32)
+        length = lengths_ref[s]
+        hit = lane == groups_ref[s]
+        mean = jnp.sum(jnp.where(hit, totals, 0.0), axis=1, keepdims=True) / GROUP
+        square = jnp.sum(jnp.where(hit, squares, 0.0), axis=1, keepdims=True) / GROUP
+        advantage = (reward - mean) / jnp.sqrt(square - mean * mean + 1.0)
+        position = lax.broadcasted_iota(jnp.int32, (1, seq), 1)
+        live = jnp.where(position < length, 1.0, 0.0)
+        scale = advantage * live / jnp.full((1, seq), length.astype(jnp.float32))
+        at = pl.ds(s * seq, seq)
+        other = cot_t[pl.ds(pl.multiple_of((1 - c) * half, 8), half), at]
+        own = cot_t[pl.ds(pl.multiple_of(c * half, 8), half), at]
+        scaled[0:half, at] = (other * scale).astype(jnp.bfloat16)
+        scaled[half:cols, at] = (own * scale).astype(jnp.bfloat16)
+
+    steps = len(OFFSETS)
+    pair_copies = [
+        remote(pair_out.at[k], pair_in.at[k], p_send.at[k], p_recv.at[k], sibling)
+        for k in range(steps)
+    ]
+    x_copies = [
+        remote(x_out.at[k], x_in.at[k], x_send.at[k], x_recv.at[k], x_next) for k in range(steps)
+    ]
+    z_copies = [
+        remote(
+            z_out.at[k], z_in.at[k], z_send.at[k], z_recv.at[k],
+            {"dp": dp, "fsdp": (z + OFFSETS[k]) % n_fsdp, "tp": y},
+        )
+        for k in range(steps - 1)
+    ]
+
+    def multiply(k):
+        hid_copies[k].wait()
+        product = jnp.dot(scaled[...], hid[k], preferred_element_type=jnp.float32)
+        pair_out[k] = product[0:half].astype(jnp.bfloat16)
+        mine[k] = product[half:cols]
+        pair_copies[k].start()
+
+    def combine(k):
+        pair_copies[k].wait_recv()
+        there = pl.ds(pl.multiple_of((1 - x) * pair, LANES), pair)
+        here = pl.ds(pl.multiple_of(x * pair, LANES), pair)
+        x_out[k] = (mine[k, :, there] + pair_in[k, :, there].astype(jnp.float32)).astype(jnp.bfloat16)
+        x_copies[k].start()
+        x_mine[k] = mine[k, :, here] + pair_in[k, :, here].astype(jnp.float32)
+
+    multiply(0)
+    for k in range(1, steps):
+        multiply(k)
+        combine(k - 1)
+    combine(steps - 1)
+
+    mast_copy.wait()
+    m_copy = remote(mast.at[c], mast.at[c], m_send, m_recv, sibling)
+    m_copy.start()
+    m_copy.wait_recv()
+    mast_t[...] = mast[...].reshape(pair, cols).T
+
+    for k in range(steps - 1):
+        x_copies[k].wait_recv()
+        z_out[k] = (x_mine[k] + x_in[k].astype(jnp.float32)).astype(jnp.bfloat16)
+        z_copies[k].start()
+    x_copies[steps - 1].wait_recv()
+    result = x_mine[steps - 1] + x_in[steps - 1].astype(jnp.float32)
+    for k in range(steps - 1):
+        z_copies[k].wait_recv()
+        result += z_in[k].astype(jnp.float32)
+    updated = mast_t[pl.ds(pl.multiple_of(c * half, 8), half)] - 0.1 * result
+    place = y * 2 + c
+    gathered[x, place] = updated.astype(jnp.bfloat16)
+
+    cut = (pair // LANES + 1) // 2 * LANES
+    parts = (pl.ds(0, cut), pl.ds(cut, pair - cut))
+
+    def spread(at_x, at_place, part, sem, where):
+        ref = gathered.at[at_x, at_place, :, parts[part]]
+        return remote(ref, ref, g_send.at[sem], g_recv.at[sem], where)
+
+    y_place = (1 - y) * 2 + c
+    to_x = [spread(x, place, p, p, x_next) for p in range(2)]
+    to_y = [spread(x, place, p, 2 + p, y_next) for p in range(2)]
+    to_sib = [spread(x, place, p, 4 + p, sibling) for p in range(2)]
+    far_y = spread(1 - x, place, 0, 6, y_next)
+    far_x = spread(x, y_place, 1, 7, x_next)
+    relay_x = [spread(1 - x, place, p, 8 + p, sibling) for p in range(2)]
+    relay_y = [spread(x, y_place, p, 10 + p, sibling) for p in range(2)]
+    relay_far = [spread(1 - x, y_place, p, 12 + p, sibling) for p in range(2)]
+    to_x[0].start()
+    to_y[1].start()
+    to_x[1].start()
+    to_y[0].start()
+    to_sib[0].start()
+    to_sib[1].start()
+    full[c] = result
+    f_copy = remote(full.at[c], full.at[c], f_send, f_recv, sibling)
+    f_copy.start()
+    to_x[0].wait_recv()
+    far_y.start()
+    relay_x[0].start()
+    to_y[1].wait_recv()
+    far_x.start()
+    relay_y[1].start()
+    f_copy.wait_recv()
+    full_t[...] = full[...].reshape(cols, pair).T
+    grad_ref[0] = full_t[pl.ds(pl.multiple_of(c * own_rows, 8), own_rows)]
+    to_x[1].wait_recv()
+    relay_x[1].start()
+    to_y[0].wait_recv()
+    relay_y[0].start()
+
+    def place_rows(at_x):
+        rows = pl.ds(pl.multiple_of(at_x * pair, 16), pair)
+        roll_ref[0, rows, :] = gathered[at_x].reshape(2 * cols, pair).T
+
+    far_y.wait_recv()
+    relay_far[0].start()
+    for copy in (to_sib[0], to_sib[1], relay_y[0], relay_y[1]):
+        copy.wait_recv()
+    place_rows(x)
+    far_x.wait_recv()
+    relay_far[1].start()
+    for copy in (relay_x[0], relay_x[1], relay_far[0], relay_far[1]):
+        copy.wait_recv()
+    place_rows(1 - x)
+
+    sent = stat_copies + pair_copies + x_copies + z_copies + to_x + to_y + to_sib
+    sent += relay_x + relay_y + relay_far + [far_y, far_x, m_copy, f_copy]
+    for copy in sent:
+        copy.wait_send()
+
+
+def fused_shards(hidden, cotangent, rewards, groups, lengths, master):
+    n_dp, n_fsdp, n_tp = lax.axis_size("dp"), lax.axis_size("fsdp"), lax.axis_size("tp")
+    tokens, width = hidden.shape
+    cols = cotangent.shape[1]
+    half = cols // 2
+    chunk = width // n_fsdp
+    pair = chunk // 2
+    own_rows = master.shape[1]
+    steps = len(OFFSETS)
+    dma, f32, bf16 = pltpu.SemaphoreType.DMA, jnp.float32, jnp.bfloat16
+    smem = pl.BlockSpec(memory_space=pltpu.SMEM)
+    anywhere = pl.BlockSpec(memory_space=pl.ANY)
+    vmem = pl.BlockSpec(memory_space=pltpu.VMEM)
+    peers = n_dp * n_fsdp
+    return pl.pallas_call(
+        functools.partial(fused_kernel, n_dp, n_fsdp, n_tp),
+        out_shape=(
+            jax.ShapeDtypeStruct((1, own_rows, cols), f32),
+            jax.ShapeDtypeStruct((1, chunk, cols * n_tp), bf16),
+        ),
+        in_specs=[smem, smem, smem, anywhere, anywhere, anywhere],
+        out_specs=(vmem, vmem),
+        scratch_shapes=[
+            pltpu.VMEM((steps, tokens, chunk), bf16),
+            pltpu.VMEM((tokens, cols), bf16),
+            pltpu.VMEM((2, own_rows, cols), f32),
+            pltpu.VMEM((cols, tokens), f32),
+            pltpu.VMEM((cols, tokens), bf16),
+            pltpu.VMEM((peers, 8, LANES), f32),
+            pltpu.VMEM((steps, half, chunk), f32),
+            pltpu.VMEM((steps, half, chunk), bf16),
+            pltpu.VMEM((steps, half, chunk), bf16),
+            pltpu.VMEM((steps, half, pair), f32),
+            pltpu.VMEM((steps, half, pair), bf16),
+            pltpu.VMEM((steps, half, pair), bf16),
+            pltpu.VMEM((steps, half, pair), bf16),
+            pltpu.VMEM((steps, half, pair), bf16),
+            pltpu.VMEM((cols, pair), f32),
+            pltpu.VMEM((2, half, pair), f32),
+            pltpu.VMEM((pair, cols), f32),
+            pltpu.VMEM((2, 2 * n_tp, half, pair), bf16),
+            dma((steps,)), dma, dma, dma((peers,)), dma((peers,)), dma, dma,
+            dma((steps,)), dma((steps,)), dma((steps,)), dma((steps,)), dma((steps,)),
+            dma((steps,)), dma, dma, dma((14,)), dma((14,)),
+        ],
+        compiler_params=pltpu.CompilerParams(
+            collective_id=0, has_side_effects=True, vmem_limit_bytes=60 * 1024 * 1024
+        ),
+    )(rewards, groups, lengths, hidden, cotangent, master)
+
+
+def fits(mesh, hidden, cotangent, rewards, groups, lengths, master):
+    n_dp, n_fsdp, n_tp = mesh.shape["dp"], mesh.shape["fsdp"], mesh.shape["tp"]
+    if (n_dp, n_fsdp, n_tp) != (4, len(OFFSETS), 2):
+        return False
+    rows_of_chip = hidden.shape[1] // n_fsdp // 2
+    half = cotangent.shape[1] // n_tp // 2
+    seq = hidden.shape[0] // rewards.shape[0]
+    aligned = rows_of_chip % LANES == 0 and half % 16 == 0 and seq % LANES == 0
+    return aligned and rewards.shape[0] // GROUP <= LANES
+
+
 def solution(mesh):
     placed = (
         P(("dp", "fsdp"), None),
@@ -60,10 +337,14 @@
         P(("dp", "fsdp")),
         P("fsdp", "dp", "tp"),
     )
-    return jax.shard_map(
-        shards,
-        mesh=mesh,
-        in_specs=placed,
-        out_specs=(P("fsdp", "dp", "tp"), P("fsdp", None, None)),
-        check_vma=False,
-    )
+
+    def step(*args):
+        return jax.shard_map(
+            fused_shards if fits(mesh, *args) else shards,
+            mesh=mesh,
+            in_specs=placed,
+            out_specs=(P("fsdp", "dp", "tp"), P("fsdp", None, None)),
+            check_vma=False,
+        )(*args)
+
+    return step

time: 289 us -> 69.2 us (0.24)
  waiting for transfers between devices: 200 us -> 0 us
  Pallas kernels: 0 us -> 57.3 us
  blocking collectives: 44.4 us -> 0 us
  between operations: 13.8 us -> 0.64 us
  local copies, waits for them, and re-layouts: 20.2 us -> 10.3 us
  matrix products: 8.94 us -> 0 us
    reduce_scatter x1 -> x0, waiting for transfers between devices: 140 us -> none  [shards(): lax.psum_scatter(product.reshape(1 * lax.axis_size('fsdp'), block_rows, c...]
    pallas_call x0 -> x1, Pallas kernels: none -> 57.3 us  [fused_shards(): pl.pallas_call(functools.partial(fused_kernel, n_dp, n_fsdp, n_tp), out_s...]
    unnamed x4 -> x0, waiting for transfers between devices: 36.1 us -> none
    psum x1 -> x0, blocking collectives: 35.1 us -> none  [shards(): lax.psum((exact_dot(reward_f, local_onehot), exact_dot(reward_f * reward_...]
    all_gather x1 -> x0, waiting for transfers between devices: 23.8 us -> none  [shards(): rollout = lax.all_gather(full_rows, 'dp', axis=1, tiled=True)]
    unnamed x9 -> x2, local copies, waits for them, and re-layouts: 15.3 us -> 4.04 us
    all_gather x1 -> x0, blocking collectives: 9.24 us -> none  [shards(): full_rows = lax.all_gather(updated, 'tp', axis=2, tiled=True)]
    dot_general x5 -> x0, matrix products: 8.94 us -> none  [the longest x1 5.51 us: shards(): jnp.einsum('td,tc->dc', hidden, weighted, preferred_element_type=jnp.floa...]
  transfers between devices with their start and end apart: 3 -> 0, of which waited for: 3 -> 0; matrix products, arithmetic and copies ran while one was open for 0% -> 0% of each run, Pallas kernels for 0% -> 0%
where the time goes in v1:
time: 69.2 us; the launch traced here: 68.3 us
  Pallas kernels  57.3 us (83%)
  local copies, waits for them, and re-layouts  10.3 us (15%)
    pallas_call x1, Pallas kernels, fused_shards(): pl.pallas_call(functools.partial(fused_kernel, n_dp, n_fsdp, n_tp), out_s...  57.3 us
    pallas_call x2, local copies, waits for them, and re-layouts, fused_shards(): pl.pallas_call(functools.partial(fused_kernel, n_dp, n_fsdp, n_tp), out_s...  6.27 us
    unnamed x2, local copies, waits for them, and re-layouts  4.04 us

profile of v1, /device:TPU:0, one launch (start us, length us, event | category | flops | bytes accessed | tf_op | source)
XLA Modules:
  0.0 68.3 jit_solution(16112679053332470694)
XLA Ops:
  0.6 1.9 %copy.8.cot_ref = bf16[512,288]{1,0:T(8,128)(2,1)} copy(bf16[512,288]{0,1:T(8,128)(2,1)} %param.7) | data formatting | bytes 589824 | tf_op args[1]
  2.5 2.2 %copy.9.master_ref = f32[1,448,288]{2,1,0:T(8,128)} copy(f32[1,448,288]{1,2,0:T(8,128)} %param.11) | data formatting | bytes 1032192 | tf_op args[5]
  4.7 57.3 %shard_map.77 = (f32[1,448,288]{2,1,0:T(8,128)}, bf16[1,1792,576]{2,1,0:T(8,128)(2,1)}) custom-call(s32[4]{0:T(128)} %rewards_ref.1, s32[4]{0:T(128)} %groups_ref.1, s32[4]{0:T(128)} %lengths_ref.1, bf16[512,7168]{1,0:T(8,128)(2,1)} %hidden_ref.1, bf16[512,288]{1,0:T(8,128)(2,1)} %copy.8.cot_ref, f32[1,448,288]{2,1,0:T(8,128)} %copy.9.master_ref), custom_call_target="tpu_custom_call" | custom-call | tf_op jit(solution)/shard_map/pallas_call | solution.py:283
  62.0 2.2 %copy.10 = f32[1,448,288]{1,2,0:T(8,128)} copy(f32[1,448,288]{2,1,0:T(8,128)} %get-tuple-element.2) | data formatting | bytes 1032192 | tf_op jit(solution)/shard_map/pallas_call | solution.py:283
  64.2 4.1 %copy.11 = bf16[1,1792,576]{1,2,0:T(8,128)(2,1)} copy(bf16[1,1792,576]{2,1,0:T(8,128)(2,1)} %get-tuple-element.3) | data formatting | bytes 4128768 | tf_op jit(solution)/shard_map/pallas_call | solution.py:283

commit v2 on v0

--- a/solution.py
+++ b/solution.py
@@ -1,6 +1,10 @@
+import functools
+
 import jax
 import jax.numpy as jnp
 from jax import lax
+from jax.experimental import pallas as pl
+from jax.experimental.pallas import tpu as pltpu
 from jax.sharding import PartitionSpec as P
 
 D = 7168
@@ -51,6 +55,322 @@
     return (owned, rollout)
 
 
+STEPS = 4
+LANES = 128
+MESH = pl.DeviceIdType.MESH
+
+
+def fused_kernel(
+    n_dp, n_fsdp, n_tp,
+    rewards_ref, groups_ref, lengths_ref, hidden_ref, cot_ref, master_ref,
+    grad_ref, roll_ref,
+    hid, cot, mast, wide, scaled, stats, mine, pair_out, pair_in, x_out, x_in,
+    z_out, z_in, full, gathered,
+    hid_sem, cot_sem, mast_sem, st_send, st_recv, m_send, m_recv, p_send, p_recv,
+    x_send, x_recv, z_send, z_recv, f_send, f_recv, g_send, g_recv, o_sem,
+):
+    dp, z, y = lax.axis_index("dp"), lax.axis_index("fsdp"), lax.axis_index("tp")
+    x, c = dp // 2, dp % 2
+    sibling = {"dp": x * 2 + (1 - c), "fsdp": z, "tp": y}
+    x_next = {"dp": (1 - x) * 2 + c, "fsdp": z, "tp": y}
+    y_next = {"dp": dp, "fsdp": z, "tp": 1 - y}
+    blocks = (n_fsdp - 1 - z, (z + n_fsdp // 2) % n_fsdp, z + 1 - 2 * (z % 2), z)
+    samples = rewards_ref.shape[0]
+    cols, tokens = cot.shape
+    half = cols // 2
+    seq = tokens // samples
+    chunk = hid.shape[2]
+    pair = chunk // 2
+    own_rows = pair // 2
+    cut = (pair // LANES + 1) // 2 * LANES
+    parts = ((0, cut), (cut, pair - cut))
+    f32, bf16 = jnp.float32, jnp.bfloat16
+
+    def remote(src, dst, send, recv, where):
+        return pltpu.make_async_remote_copy(
+            src_ref=src, dst_ref=dst, send_sem=send, recv_sem=recv,
+            device_id=where, device_id_type=MESH,
+        )
+
+    def side(of_x, p):
+        low, wide_by = parts[p]
+        return pl.ds(pl.multiple_of(of_x * pair + low, LANES), wide_by)
+
+    def lanes(p):
+        return pl.ds(*parts[p])
+
+    peers = [
+        (i * n_fsdp + j, {"dp": (dp + i) % n_dp, "fsdp": (z + j) % n_fsdp, "tp": y})
+        for i in range(n_dp) for j in range(n_fsdp) if i or j
+    ]
+    barrier = pltpu.get_barrier_semaphore()
+    for _, where in peers:
+        pl.semaphore_signal(barrier, inc=1, device_id=where, device_id_type=MESH)
+    pl.semaphore_signal(barrier, inc=1, device_id=y_next, device_id_type=MESH)
+
+    cot_copy = pltpu.make_async_copy(cot_ref, cot, cot_sem)
+    cot_copy.start()
+    hid_copies = []
+    for k in range(STEPS):
+        start = pl.multiple_of(blocks[k] * chunk, LANES)
+        hid_copies.append(
+            pltpu.make_async_copy(hidden_ref.at[:, pl.ds(start, chunk)], hid.at[k], hid_sem.at[k])
+        )
+        hid_copies[-1].start()
+    mast_copy = pltpu.make_async_copy(master_ref, mast.at[c], mast_sem)
+    mast_copy.start()
+
+    lane = lax.broadcasted_iota(jnp.int32, (1, LANES), 1)
+    total_row = jnp.zeros((1, LANES), f32)
+    square_row = jnp.zeros((1, LANES), f32)
+    for s in range(samples):
+        reward = rewards_ref[s].astype(f32)
+        hit = lane == groups_ref[s]
+        total_row += jnp.where(hit, reward, 0.0)
+        square_row += jnp.where(hit, reward * reward, 0.0)
+    row = lax.broadcasted_iota(jnp.int32, (8, LANES), 0)
+    stats[0] = jnp.where(row == 0, total_row, jnp.where(row == 1, square_row, 0.0))
+
+    pl.semaphore_wait(barrier, len(peers) + 1)
+    stat_copies = []
+    for slot, where in peers:
+        stat_copies.append(remote(stats.at[0], stats.at[slot], st_send.at[slot], st_recv.at[slot], where))
+        stat_copies[-1].start()
+
+    mast_copy.wait()
+    other_half = pl.ds(pl.multiple_of((1 - c) * half, 8), half)
+    own_half = pl.ds(pl.multiple_of(c * half, 8), half)
+    m_copy = remote(mast.at[c, other_half], mast.at[c, other_half], m_send, m_recv, sibling)
+    m_copy.start()
+
+    cot_copy.wait()
+    for copy in stat_copies:
+        copy.wait_recv()
+    summed = stats[0]
+    for slot, _ in peers:
+        summed += stats[slot]
+    totals, squares = summed[0:1], summed[1:2]
+    for s in range(samples):
+        reward = rewards_ref[s].astype(f32)
+        length = lengths_ref[s]
+        hit = lane == groups_ref[s]
+        mean = jnp.sum(jnp.where(hit, totals, 0.0), axis=1, keepdims=True) / GROUP
+        square = jnp.sum(jnp.where(hit, squares, 0.0), axis=1, keepdims=True) / GROUP
+        advantage = (reward - mean) / jnp.sqrt(square - mean * mean + 1.0)
+        position = lax.broadcasted_iota(jnp.int32, (1, seq), 1)
+        live = jnp.where(position < length, 1.0, 0.0)
+        scale = advantage * live / jnp.full((1, seq), length.astype(f32))
+        at = pl.ds(s * seq, seq)
+        top = (cot[0:half, at].astype(f32) * scale).astype(bf16)
+        low = (cot[half:cols, at].astype(f32) * scale).astype(bf16)
+        scaled[pl.ds(pl.multiple_of(c * half, 16), half), at] = low
+        scaled[pl.ds(pl.multiple_of((1 - c) * half, 16), half), at] = top
+
+    def pair_copy(k, p, at, of_x):
+        ref = (k, slice(None), side(of_x, p))
+        sem = (k * 2 + p) * 2 + at
+        return remote(pair_out.at[ref], pair_in.at[ref], p_send.at[sem], p_recv.at[sem], sibling)
+
+    units = [(p, k) for p in range(2) for k in range(STEPS)]
+    sent = []
+    pairs, x_copies, z_copies = {}, {}, {}
+    for p, k in units:
+        pairs[p, k] = (pair_copy(k, p, 0, 1 - x), pair_copy(k, p, 1, x))
+        ref = (k, slice(None), lanes(p))
+        x_copies[p, k] = remote(
+            x_out.at[ref], x_in.at[ref], x_send.at[k * 2 + p], x_recv.at[k * 2 + p], x_next
+        )
+        sent += [*pairs[p, k], x_copies[p, k]]
+        if k < STEPS - 1:
+            z_copies[p, k] = remote(
+                z_out.at[ref], z_in.at[ref], z_send.at[k * 2 + p], z_recv.at[k * 2 + p],
+                {"dp": dp, "fsdp": blocks[k], "tp": y},
+            )
+            sent.append(z_copies[p, k])
+
+    def multiply(p, k, at):
+        if p == 0 and at == 0:
+            hid_copies[k].wait()
+        columns = side(x if at else 1 - x, p)
+        product = jnp.dot(scaled[...], hid[k, :, columns], preferred_element_type=f32)
+        pair_out[k, :, columns] = product[0:half].astype(bf16)
+        mine[k, :, columns] = product[half:cols]
+        pairs[p, k][at].start()
+
+    def combine(p, k):
+        pairs[p, k][0].wait_recv()
+        columns = side(1 - x, p)
+        total = mine[k, :, columns] + pair_in[k, :, columns].astype(f32)
+        x_out[k, :, lanes(p)] = total.astype(bf16)
+        x_copies[p, k].start()
+
+    def reduced(p, k):
+        pairs[p, k][1].wait_recv()
+        columns = side(x, p)
+        total = mine[k, :, columns] + pair_in[k, :, columns].astype(f32)
+        x_copies[p, k].wait_recv()
+        return total + x_in[k, :, lanes(p)].astype(f32)
+
+    def forward(p, k):
+        z_out[k, :, lanes(p)] = reduced(p, k).astype(bf16)
+        z_copies[p, k].start()
+
+    multiply(0, 0, 0)
+    for n, (p, k) in enumerate(units):
+        multiply(p, k, 1)
+        if n + 1 < len(units):
+            multiply(*units[n + 1], 0)
+        combine(p, k)
+        if n == 5:
+            forward(0, 0)
+
+    m_copy.wait_recv()
+    first, second = mast[0, own_half, :], mast[1, own_half, :]
+    wide[...] = jnp.concatenate([first, second], axis=1)
+
+    place, y_place = y * 2 + c, (1 - y) * 2 + c
+
+    def rows(at_place):
+        return pl.ds(pl.multiple_of(at_place * half, 16), half)
+
+    def spread(p, sem, at_x, at_place, where):
+        ref = gathered.at[rows(at_place), side(at_x, p)]
+        return remote(ref, ref, g_send.at[p * 8 + sem], g_recv.at[p * 8 + sem], where)
+
+    def relay(p, sem, at_x, at_place):
+        ref = (rows(at_place), side(at_x, p))
+        return remote(
+            gathered.at[ref], roll_ref.at[ref],
+            g_send.at[p * 8 + sem], g_recv.at[p * 8 + sem], sibling,
+        )
+
+    def write(p, sem, at_x, at_place):
+        ref = (rows(at_place), side(at_x, p))
+        return pltpu.make_async_copy(gathered.at[ref], roll_ref.at[ref], o_sem.at[p * 4 + sem])
+
+    sites = ((x, place), (1 - x, place), (x, y_place), (1 - x, y_place))
+    to_x = [spread(p, 0, x, place, x_next) for p in range(2)]
+    to_y = [spread(p, 1, x, place, y_next) for p in range(2)]
+    far = [spread(p, 2, 1 - x, place, y_next) for p in range(2)]
+    relays = [[relay(p, 3 + i, *sites[i]) for i in range(4)] for p in range(2)]
+    writes = [[write(p, i, *sites[i]) for i in range(4)] for p in range(2)]
+    f_copies = [
+        remote(full.at[c, :, lanes(p)], full.at[c, :, lanes(p)], f_send.at[p], f_recv.at[p], sibling)
+        for p in range(2)
+    ]
+
+    def finish(p):
+        result = reduced(p, STEPS - 1)
+        for k in range(STEPS - 1):
+            z_copies[p, k].wait_recv()
+            result += z_in[k, :, lanes(p)].astype(f32)
+        gathered[rows(place), side(x, p)] = (wide[:, lanes(p)] - 0.1 * result).astype(bf16)
+        full[c, :, lanes(p)] = result
+        to_x[p].start()
+        to_y[p].start()
+        f_copies[p].start()
+        relays[p][0].start()
+        writes[p][0].start()
+
+    def pass_on(p, i):
+        relays[p][i].start()
+        writes[p][i].start()
+
+    for k in range(1, STEPS - 1):
+        forward(0, k)
+    forward(1, 0)
+    finish(0)
+    forward(1, 1)
+    to_y[0].wait_recv()
+    pass_on(0, 2)
+    forward(1, 2)
+    finish(1)
+    to_x[0].wait_recv()
+    far[0].start()
+    pass_on(0, 1)
+    for p in range(2):
+        f_copies[p].wait_recv()
+    for i in range(2):
+        band = pl.ds(i * half, half)
+        grad_ref[band, :] = jnp.where(c == 0, full[i, :, 0:own_rows], full[i, :, own_rows:pair])
+    to_x[1].wait_recv()
+    far[1].start()
+    pass_on(1, 1)
+    to_y[1].wait_recv()
+    pass_on(1, 2)
+    for p in range(2):
+        far[p].wait_recv()
+        pass_on(p, 3)
+
+    for p in range(2):
+        for i in range(4):
+            relays[p][i].wait_recv()
+            writes[p][i].wait()
+        sent += [*relays[p], to_x[p], to_y[p], far[p], f_copies[p]]
+    for copy in sent + stat_copies + [m_copy]:
+        copy.wait_send()
+
+
+def fused_shards(hidden, cotangent, rewards, groups, lengths, master):
+    n_dp, n_fsdp, n_tp = lax.axis_size("dp"), lax.axis_size("fsdp"), lax.axis_size("tp")
+    tokens, width = hidden.shape
+    cols = cotangent.shape[1]
+    half = cols // 2
+    chunk = width // n_fsdp
+    pair = chunk // 2
+    own_rows = master.shape[1]
+    dma, f32, bf16 = pltpu.SemaphoreType.DMA, jnp.float32, jnp.bfloat16
+    smem = pl.BlockSpec(memory_space=pltpu.SMEM)
+    anywhere = pl.BlockSpec(memory_space=pl.ANY)
+    vmem = pl.BlockSpec(memory_space=pltpu.VMEM)
+    peers = n_dp * n_fsdp
+    grad, roll = pl.pallas_call(
+        functools.partial(fused_kernel, n_dp, n_fsdp, n_tp),
+        out_shape=(
+            jax.ShapeDtypeStruct((cols, own_rows), f32),
+            jax.ShapeDtypeStruct((cols * n_tp, chunk), bf16),
+        ),
+        in_specs=[smem, smem, smem, anywhere, anywhere, anywhere],
+        out_specs=(vmem, anywhere),
+        scratch_shapes=[
+            pltpu.VMEM((STEPS, tokens, chunk), bf16),
+            pltpu.VMEM((cols, tokens), bf16),
+            pltpu.VMEM((2, cols, own_rows), f32),
+            pltpu.VMEM((half, pair), f32),
+            pltpu.VMEM((cols, tokens), bf16),
+            pltpu.VMEM((peers, 8, LANES), f32),
+            pltpu.VMEM((STEPS, half, chunk), f32),
+            pltpu.VMEM((STEPS, half, chunk), bf16),
+            pltpu.VMEM((STEPS, half, chunk), bf16),
+            pltpu.VMEM((STEPS, half, pair), bf16),
+            pltpu.VMEM((STEPS, half, pair), bf16),
+            pltpu.VMEM((STEPS, half, pair), bf16),
+            pltpu.VMEM((STEPS, half, pair), bf16),
+            pltpu.VMEM((2, half, pair), f32),
+            pltpu.VMEM((cols * n_tp, chunk), bf16),
+            dma((STEPS,)), dma, dma, dma((peers,)), dma((peers,)), dma, dma,
+            dma((4 * STEPS,)), dma((4 * STEPS,)), dma((2 * STEPS,)), dma((2 * STEPS,)),
+            dma((2 * STEPS,)), dma((2 * STEPS,)), dma((2,)), dma((2,)), dma((16,)), dma((16,)),
+            dma((8,)),
+        ],
+        compiler_params=pltpu.CompilerParams(
+            collective_id=0, has_side_effects=True, vmem_limit_bytes=60 * 1024 * 1024
+        ),
+    )(rewards, groups, lengths, hidden, cotangent.T, master[0].T)
+    return grad.T[None], roll.T[None]
+
+
+def fits(mesh, hidden, cotangent, rewards, groups, lengths, master):
+    n_dp, n_fsdp, n_tp = mesh.shape["dp"], mesh.shape["fsdp"], mesh.shape["tp"]
+    if (n_dp, n_fsdp, n_tp) != (4, STEPS, 2):
+        return False
+    rows_of_chip = hidden.shape[1] // n_fsdp // 2
+    half = cotangent.shape[1] // n_tp // 2
+    seq = hidden.shape[0] // rewards.shape[0]
+    aligned = rows_of_chip % LANES == 0 and half % 16 == 0 and seq % LANES == 0
+    return aligned and rewards.shape[0] // GROUP <= LANES
+
+
 def solution(mesh):
     placed = (
         P(("dp", "fsdp"), None),
@@ -60,10 +380,14 @@
         P(("dp", "fsdp")),
         P("fsdp", "dp", "tp"),
     )
-    return jax.shard_map(
-        shards,
-        mesh=mesh,
-        in_specs=placed,
-        out_specs=(P("fsdp", "dp", "tp"), P("fsdp", None, None)),
-        check_vma=False,
-    )
+
+    def step(*args):
+        return jax.shard_map(
+            fused_shards if fits(mesh, *args) else shards,
+            mesh=mesh,
+            in_specs=placed,
+            out_specs=(P("fsdp", "dp", "tp"), P("fsdp", None, None)),
+            check_vma=False,
+        )(*args)
+
+    return step

time: 289 us -> 60.6 us (0.21)
  waiting for transfers between devices: 200 us -> 0 us
  Pallas kernels: 0 us -> 54.8 us
  blocking collectives: 44.4 us -> 0 us
  local copies, waits for them, and re-layouts: 20.2 us -> 4.93 us
  between operations: 13.8 us -> 0.64 us
  matrix products: 8.94 us -> 0 us
    reduce_scatter x1 -> x0, waiting for transfers between devices: 140 us -> none  [shards(): lax.psum_scatter(product.reshape(1 * lax.axis_size('fsdp'), block_rows, c...]
    pallas_call x0 -> x1, Pallas kernels: none -> 54.8 us  [fused_shards(): pl.pallas_call(functools.partial(fused_kernel, n_dp, n_fsdp, n_tp), out_s...]
    unnamed x4 -> x0, waiting for transfers between devices: 36.1 us -> none
    psum x1 -> x0, blocking collectives: 35.1 us -> none  [shards(): lax.psum((exact_dot(reward_f, local_onehot), exact_dot(reward_f * reward_...]
    all_gather x1 -> x0, waiting for transfers between devices: 23.8 us -> none  [shards(): rollout = lax.all_gather(full_rows, 'dp', axis=1, tiled=True)]
    unnamed x9 -> x2, local copies, waits for them, and re-layouts: 15.3 us -> 4.93 us
    all_gather x1 -> x0, blocking collectives: 9.24 us -> none  [shards(): full_rows = lax.all_gather(updated, 'tp', axis=2, tiled=True)]
    dot_general x5 -> x0, matrix products: 8.94 us -> none  [the longest x1 5.51 us: shards(): jnp.einsum('td,tc->dc', hidden, weighted, preferred_element_type=jnp.floa...]
  transfers between devices with their start and end apart: 3 -> 0, of which waited for: 3 -> 0; matrix products, arithmetic and copies ran while one was open for 0% -> 0% of each run, Pallas kernels for 0% -> 0%
where the time goes in v2:
time: 60.6 us; the launch traced here: 60.4 us
  Pallas kernels  54.8 us (90%)
  local copies, waits for them, and re-layouts  4.93 us (8%)
  between operations  0.64 us (1%)
    pallas_call x1, Pallas kernels, fused_shards(): pl.pallas_call(functools.partial(fused_kernel, n_dp, n_fsdp, n_tp), out_s...  54.8 us
    unnamed x2, local copies, waits for them, and re-layouts  4.93 us

profile of v2, /device:TPU:0, one launch (start us, length us, event | category | flops | bytes accessed | tf_op | source)
XLA Modules:
  0.0 60.4 jit_solution(16860395718634239948)
XLA Ops:
  0.6 54.8 %shard_map.77 = (f32[288,448]{1,0:T(8,128)}, bf16[576,1792]{1,0:T(8,128)(2,1)}) custom-call(s32[4]{0:T(128)} %rewards_ref.1, s32[4]{0:T(128)} %groups_ref.1, s32[4]{0:T(128)} %lengths_ref.1, bf16[512,7168]{1,0:T(8,128)(2,1)} %hidden_ref.1, bf16[288,512]{1,0:T(8,128)(2,1)} %bitcast.13, f32[288,448]{1,0:T(8,128)} %bitcast.11), custom_call_target="tpu_custom_call" | custom-call | tf_op jit(solution)/shard_map/pallas_call | solution.py:327
  55.4 1.9 %copy.10 = f32[1,448,288]{1,2,0:T(8,128)} copy(f32[1,448,288]{1,2,0:T(8,128)} %bitcast.12) | data formatting | bytes 1032192
  57.4 3.0 %copy.11 = bf16[1,1792,576]{1,2,0:T(8,128)(2,1)} copy(bf16[1,1792,576]{1,2,0:T(8,128)(2,1)} %bitcast.10) | data formatting | bytes 4128768

commit v3 on v2

--- a/solution.py
+++ b/solution.py
@@ -82,7 +82,7 @@
     chunk = hid.shape[2]
     pair = chunk // 2
     own_rows = pair // 2
-    cut = (pair // LANES + 1) // 2 * LANES
+    cut = pair // LANES * 3 // 4 * LANES
     parts = ((0, cut), (cut, pair - cut))
     f32, bf16 = jnp.float32, jnp.bfloat16
 
@@ -221,8 +221,10 @@
         if n + 1 < len(units):
             multiply(*units[n + 1], 0)
         combine(p, k)
-        if n == 5:
+        if n == 4:
             forward(0, 0)
+        if n == 6:
+            forward(0, 1)
 
     m_copy.wait_recv()
     first, second = mast[0, own_half, :], mast[1, own_half, :]
@@ -251,7 +253,16 @@
     sites = ((x, place), (1 - x, place), (x, y_place), (1 - x, y_place))
     to_x = [spread(p, 0, x, place, x_next) for p in range(2)]
     to_y = [spread(p, 1, x, place, y_next) for p in range(2)]
-    far = [spread(p, 2, 1 - x, place, y_next) for p in range(2)]
+    far = [spread(0, 2, 1 - x, place, y_next)]
+    low_lane, tail = parts[1][0], parts[1][1] // 2
+    by_y = (rows(place), pl.ds(pl.multiple_of((1 - x) * pair + low_lane, LANES), tail))
+    by_x = (rows(y_place), pl.ds(pl.multiple_of(x * pair + low_lane + tail, LANES), tail))
+    far.append(
+        remote(gathered.at[by_y], gathered.at[by_y], g_send.at[10], g_recv.at[10], y_next)
+    )
+    far.append(
+        remote(gathered.at[by_x], gathered.at[by_x], g_send.at[7], g_recv.at[7], x_next)
+    )
     relays = [[relay(p, 3 + i, *sites[i]) for i in range(4)] for p in range(2)]
     writes = [[write(p, i, *sites[i]) for i in range(4)] for p in range(2)]
     f_copies = [
@@ -276,18 +287,17 @@
         relays[p][i].start()
         writes[p][i].start()
 
-    for k in range(1, STEPS - 1):
-        forward(0, k)
+    forward(0, 2)
     forward(1, 0)
+    forward(1, 1)
     finish(0)
-    forward(1, 1)
-    to_y[0].wait_recv()
-    pass_on(0, 2)
     forward(1, 2)
-    finish(1)
     to_x[0].wait_recv()
     far[0].start()
     pass_on(0, 1)
+    to_y[0].wait_recv()
+    pass_on(0, 2)
+    finish(1)
     for p in range(2):
         f_copies[p].wait_recv()
     for i in range(2):
@@ -297,17 +307,20 @@
     far[1].start()
     pass_on(1, 1)
     to_y[1].wait_recv()
+    far[2].start()
     pass_on(1, 2)
-    for p in range(2):
-        far[p].wait_recv()
-        pass_on(p, 3)
+    far[0].wait_recv()
+    pass_on(0, 3)
+    far[1].wait_recv()
+    far[2].wait_recv()
+    pass_on(1, 3)
 
     for p in range(2):
         for i in range(4):
             relays[p][i].wait_recv()
             writes[p][i].wait()
-        sent += [*relays[p], to_x[p], to_y[p], far[p], f_copies[p]]
-    for copy in sent + stat_copies + [m_copy]:
+        sent += [*relays[p], to_x[p], to_y[p], f_copies[p]]
+    for copy in sent + far + stat_copies + [m_copy]:
         copy.wait_send()
 
 
@@ -367,7 +380,7 @@
     rows_of_chip = hidden.shape[1] // n_fsdp // 2
     half = cotangent.shape[1] // n_tp // 2
     seq = hidden.shape[0] // rewards.shape[0]
-    aligned = rows_of_chip % LANES == 0 and half % 16 == 0 and seq % LANES == 0
+    aligned = rows_of_chip % (7 * LANES) == 0 and half % 16 == 0 and seq % LANES == 0
     return aligned and rewards.shape[0] // GROUP <= LANES
 
 

time: 60.6 us -> 64.4 us (1.063)
  Pallas kernels: 54.8 us -> 58.6 us
    pallas_call x1, Pallas kernels: 54.8 us -> 58.6 us  [fused_shards(): pl.pallas_call(functools.partial(fused_kernel, n_dp, n_fsdp, n_tp), out_s...]
where the time goes in v3:
time: 64.4 us; the launch traced here: 64.2 us
  Pallas kernels  58.6 us (91%)
  local copies, waits for them, and re-layouts  4.93 us (8%)
    pallas_call x1, Pallas kernels, fused_shards(): pl.pallas_call(functools.partial(fused_kernel, n_dp, n_fsdp, n_tp), out_s...  58.6 us
    unnamed x2, local copies, waits for them, and re-layouts  4.93 us

profile of v3, /device:TPU:0, one launch (start us, length us, event | category | flops | bytes accessed | tf_op | source)
XLA Modules:
  0.0 64.2 jit_solution(4646931205300846173)
XLA Ops:
  0.6 58.6 %shard_map.77 = (f32[288,448]{1,0:T(8,128)}, bf16[576,1792]{1,0:T(8,128)(2,1)}) custom-call(s32[4]{0:T(128)} %rewards_ref.1, s32[4]{0:T(128)} %groups_ref.1, s32[4]{0:T(128)} %lengths_ref.1, bf16[512,7168]{1,0:T(8,128)(2,1)} %hidden_ref.1, bf16[288,512]{1,0:T(8,128)(2,1)} %bitcast.13, f32[288,448]{1,0:T(8,128)} %bitcast.11), custom_call_target="tpu_custom_call" | custom-call | tf_op jit(solution)/shard_map/pallas_call | solution.py:340
  59.2 1.9 %copy.10 = f32[1,448,288]{1,2,0:T(8,128)} copy(f32[1,448,288]{1,2,0:T(8,128)} %bitcast.12) | data formatting | bytes 1032192
  61.2 3.0 %copy.11 = bf16[1,1792,576]{1,2,0:T(8,128)(2,1)} copy(bf16[1,1792,576]{1,2,0:T(8,128)(2,1)} %bitcast.10) | data formatting | bytes 4128768
